TPU v7x, 32 devices: a whole 2x2x4 slice. The times are simulated.
32 devices in a mesh: tile: 8 (over z, x), dir: 4 (over y, core).
Axes of the slice: x: 2, y: 2, z: 4, core: 2. Of those that a mesh axis runs over, the one named last changes fastest.
Arguments:
- layers: bfloat16 [4, 1024, 2048], P('dir', 'tile'), may hold values from -6 to 6
- offsets: int32 [4, 4, 2], replicated, may hold values from 0 to 8191, as said below
- subap_valid: int32 [8, 16], P('tile'), may hold values from 0 to 1, as said below
- defocus: float32 [3], replicated, may hold values from -0.08 to 0.08
- weights: float32 [3], replicated, may hold values from 0.25 to 1
Outputs:
- spots: bfloat16 [4, 8, 128, 2048], P('dir', 'tile')
Inputs may be any that keep to these rules, and one draw needn't show every extreme that they name: offsets[d, l, 0] < 1024 and offsets[d, l, 1] < 8192; both bounds minus one are taken by some pair in every draw. `subap_valid`: the part of an annulus of lit subapertures that falls in the strip, with a few dead ones.
All inputs are finite; a program needn't handle non-finite values.
Results may differ from a plain program's by a relative error of at most 0.0055.
Values may be sent and summed in bfloat16 or wider, within the bound.
A program may use at most 64 MiB of HBM per device.

v0:
```python
import math

import jax
import jax.numpy as jnp
from jax import lax
from jax.sharding import PartitionSpec as P

SUBPIX = 128
SPOT = 128
SUBX = 16
SLICES = 3
REACH = 2
QUANT = 4
OVER = 2
PCOLS = 2048


def shifted(value, axis, by):
    count = lax.axis_size(axis)
    return lax.ppermute(value, axis, [(i, (i + by) % count) for i in range(count)])


def tables():
    frequency = jnp.arange(SPOT, dtype=jnp.float32) - SPOT // 2
    position = jnp.arange(SUBPIX, dtype=jnp.float32) - (SUBPIX - 1) / 2.0
    phase_angle = -2.0 * math.pi / (OVER * SUBPIX) * frequency[:, None] * position[None, :]
    factor = 1.0 / math.sqrt(SUBPIX)
    real_part = jnp.cos(phase_angle) * factor
    imag_part = jnp.sin(phase_angle) * factor
    left_table = jnp.concatenate(
        [jnp.concatenate([real_part, -imag_part], 1), jnp.concatenate([imag_part, real_part], 1)], 0
    ).astype(jnp.bfloat16)
    right_table = jnp.concatenate(
        [
            jnp.concatenate([real_part.T, imag_part.T], 1),
            jnp.concatenate([-imag_part.T, real_part.T], 1),
        ],
        0,
    ).astype(jnp.bfloat16)
    return (left_table, right_table)


def interpolate(window, offset_pair):
    col_steps = offset_pair[1] // QUANT
    col_frac = (offset_pair[1] % QUANT).astype(jnp.float32) / QUANT
    row_frac = (offset_pair[0] % QUANT).astype(jnp.float32) / QUANT
    col_first = jnp.roll(window, -col_steps, axis=1)
    col_second = jnp.roll(window, -(col_steps + 1), axis=1)
    across = (1.0 - col_frac) * col_first + col_frac * col_second
    return ((1.0 - row_frac) * across[:-1] + row_frac * across[1:]).astype(jnp.bfloat16)


def spots_row(pupil_phase, first_row, total_rows, defocus, weights, valid_row):
    left_table, right_table = tables()
    row_position = (
        (first_row + jnp.arange(SUBPIX, dtype=jnp.int32)).astype(jnp.float32)
        - (total_rows - 1) / 2.0
    ) / SUBPIX
    col_position = (jnp.arange(PCOLS, dtype=jnp.float32) - (PCOLS - 1) / 2.0) / SUBPIX
    radius = row_position[:, None] ** 2 + col_position[None, :] ** 2
    spot_sum = jnp.zeros((SPOT * SUBX, SPOT), jnp.float32)
    for altitude in range(SLICES):
        phase_angle = pupil_phase + defocus[altitude] * radius
        pupil_field = jnp.concatenate([jnp.cos(phase_angle), jnp.sin(phase_angle)], 0).astype(
            jnp.bfloat16
        )
        focal_plane = jnp.dot(left_table, pupil_field, preferred_element_type=jnp.float32).astype(
            jnp.bfloat16
        )
        blocks = jnp.concatenate(
            [
                focal_plane[:SPOT].reshape(SPOT * SUBX, SUBPIX),
                focal_plane[SPOT:].reshape(SPOT * SUBX, SUBPIX),
            ],
            1,
        )
        spot_field = jnp.dot(blocks, right_table, preferred_element_type=jnp.float32)
        spot_sum = spot_sum + weights[altitude] * (
            spot_field[:, :SPOT] ** 2 + spot_field[:, SPOT:] ** 2
        )
    scaled = spot_sum / jnp.sum(weights)
    masked = scaled.reshape(SPOT, SUBX, SPOT) * valid_row.astype(jnp.float32)[None, :, None]
    return masked.reshape(SPOT, SUBX * SPOT).astype(jnp.bfloat16)


def extend(block):
    pieces = [block]
    for distance in range(1, REACH + 1):
        pieces.append(shifted(block, "tile", -distance))
    return jnp.concatenate(pieces, 1)


def shifted_term(extended, offset_pair):
    window = lax.dynamic_slice_in_dim(extended, offset_pair[0] // QUANT, SUBPIX + 1, 0).astype(
        jnp.float32
    )
    return interpolate(window, offset_pair)


def shards(layers, offsets, subap_valid, defocus, weights):
    own_dir = lax.axis_index("dir")
    tile_index = lax.axis_index("tile")
    total_rows = lax.axis_size("tile") * SUBPIX
    pupil_phase = jnp.zeros((SUBPIX, PCOLS), jnp.float32)
    extended = extend(layers)
    offset_pairs = lax.dynamic_index_in_dim(offsets, own_dir, 1, keepdims=False)
    own_terms = jnp.stack(
        [shifted_term(extended[0], offset_pairs[target]) for target in range(lax.axis_size("dir"))],
        0,
    )
    arrived = lax.all_to_all(own_terms, "dir", split_axis=0, concat_axis=0, tiled=True)
    for layer_index in range(arrived.shape[0]):
        pupil_phase = pupil_phase + arrived[layer_index].astype(jnp.float32)
    spots = spots_row(
        pupil_phase, tile_index * SUBPIX, total_rows, defocus, weights, subap_valid[0]
    )
    return spots[None, None]


def solution(mesh):
    placed = (P("dir", "tile", None), P(), P("tile", None), P(), P())
    return jax.shard_map(
        shards, mesh=mesh, in_specs=placed, out_specs=P("dir", "tile", None, None), check_vma=False
    )
```

profile of v0, /device:TPU:0, one launch (start us, length us, event | category | flops | bytes accessed | tf_op | source)
XLA Modules:
  0.0 96.5 jit_solution(12028041397582274564)
XLA Ops:
  0.0 6.0 %collective-permute-start = (bf16[1,128,2048]{2,1,0:T(8,128)(2,1)}, bf16[1,128,2048]{2,1,0:T(8,128)(2,1)S(1)}, u32[]{:S(2)}, u32[]{:S(2)}) collective-permute-start(bf16[1,128,2048]{2,1,0:T(8,128)(2,1)} %param.7), channel_id=1, source_target_pairs={{0,28},{4,0},{8,4},{12,8},{16,12},{20,16},{24,20},{28,24},{1,29},{... | collective-permute-start | bytes 1572872 | tf_op jit(solution)/shard_map/ppermute | solution.py:20
  6.0 0.4 collective-permute-start.1
  6.5 1.5 %constant_dynamic-slice_fusion.1 = (s32[1,1,1]{1,2,0:T(1,128)}, s32[1,1,1]{1,2,0:T(1,128)}, s32[1,1,1]{1,2,0:T(1,128)}, s32[1,1,1]{1,2,0:T(1,128)}, s32[1,1,1]{1...) fusion(s32[4,4,2]{1,2,0:T(2,128)} %param.8, s32[]{:T(128)S(6)} %select_n.85, ...), kind=kLoop, calls=%fused_computation.137 | loop fusion | bytes 80 | tf_op jit(solution)/shard_map/slice | solution.py:46
  28.3 1.1 %constant_dynamic-update-slice_fusion.2 = bf16[1,384,2048]{2,1,0:T(8,128)(2,1)S(1)} fusion(bf16[1,128,2048]{2,1,0:T(8,128)(2,1)} %param.7), kind=kLoop, calls=%fused_computation.134 | loop fusion | bytes 1048576
  29.6 0.7 bitcast_convert_fusion.3
  30.2 2.4 %fusion.12 = (f32[129,2048]{1,0:T(8,128)S(1)}, f32[129,2048]{1,0:T(8,128)S(1)}) fusion(s32[]{:T(128)S(6)} %select_n.127, f32[129,2048]{1,0:T(8,128)S(1)} %get-tuple-element.11, s32[]{:T(128)S(6)} %select_n.125, f32[]{:T(128)S(6)} %div.108, f32[]{:T(128)S(6)} %sub.103, s32[]{:T(128)S(6)} %select_n.123, f32[]{:T(128)S(6)} %div.100, s32[]{:T(128)S(6)} %select_n.121, ...), kind=kLoop, calls=%fused_computation.35 | loop fusion | flops 2641920 | bytes 4227104 | tf_op jit(solution)/shard_map/add | solution.py:49
  32.6 0.2 fusion.61
  33.1 2.4 %fusion.2 = (f32[129,2048]{1,0:T(8,128)S(1)}, f32[129,2048]{1,0:T(8,128)S(1)}) fusion(s32[]{:T(128)S(6)} %select_n.135, f32[129,2048]{1,0:T(8,128)S(1)} %get-tuple-element.9, s32[]{:T(128)S(6)} %select_n.133, f32[]{:T(128)S(6)} %div.124, f32[]{:T(128)S(6)} %sub.111, s32[]{:T(128)S(6)} %select_n.131, f32[]{:T(128)S(6)} %div.116, s32[]{:T(128)S(6)} %select_n.129, ...), kind=kLoop, calls=%fused_computation.25 | loop fusion | flops 2641920 | bytes 4227104 | tf_op jit(solution)/shard_map/add | solution.py:49
  35.9 1.6 %pad_maximum_fusion = bf16[4,128,2048]{2,1,0:T(8,128)(2,1)} fusion(bf16[1,128,2048]{2,1,0:T(8,128)(2,1)S(1)} %fusion.64, bf16[1,128,2048]{2,1,0:T(8,128)(2,1)S(1)} %fusion.63, bf16[1,128,2048]{2,1,0:T(8,128)(2,1)S(1)} %fusion.62, bf16[1,128,2048]{2,1,0:T(8,128)(2,1)S(1)} %fusion.61), kind=kLoop, calls=%fused_computation.19 | loop fusion | flops 3145728 | bytes 4194304 | tf_op jit(solution)/shard_map/stack | solution.py:107
  37.5 3.9 %all-to-all-start = ((bf16[4,128,2048]{2,1,0:T(8,128)(2,1)}), bf16[4,128,2048]{2,1,0:T(8,128)(2,1)S(1)}, u32[]{:S(2)}, u32[]{:S(2)}) async-start(bf16[4,128,2048]{2,1,0:T(8,128)(2,1)} %pad_maximum_fusion), calls=%async_computation | async-start | bytes 4194304 | tf_op jit(solution)/shard_map/all_to_all | solution.py:111
  41.4 0.7 reduce_sum.9
  42.1 0.7 fusion.86
  42.8 0.6 fusion.87
  43.5 0.6 fusion.75
  44.1 22.8 %all-to-all-done = bf16[4,128,2048]{2,1,0:T(8,128)(2,1)S(1)} async-done(((bf16[4,128,2048]{2,1,0:T(8,128)(2,1)}), bf16[4,128,2048]{2,1,0:T(8,128)(2,1)S(1)}, u32[]{:S(2)}, u32[]{:S(2)}) %all-to-all-start) | async-done | bytes 2097184 | tf_op jit(solution)/shard_map/all_to_all | solution.py:111
  66.9 4.5 %cosine_convert_fusion.2 = (bf16[128,2048]{1,0:T(8,128)(2,1)S(1)}, f32[1,128,2048]{2,1,0:T(8,128)S(1)}) fusion(f32[2048]{0:T(1024)S(1)} %multiply_multiply_fusion, f32[128]{0:T(128)S(1)} %multiply_multiply_fusion.1, f32[]{:T(128)} %bitcast.22, bf16[4,128,2048]{2,1,0:T(8,128)(2,1)S(1)} %all-to-all-done), kind=kLoop, calls=%fused_computation.104 | loop fusion | flops 2883584 | bytes 3678724 | tf_op jit(solution)/shard_map/convert.14
  71.3 13.8 %sine_convert_fusion.2 = (bf16[128,2048]{1,0:T(8,128)(2,1)S(1)}, bf16[128,2048]{1,0:T(8,128)(2,1)S(1)}, bf16[128,2048]{1,0:T(8,128)(2,1)S(1)}, bf16[128,2048]{1,0:T(8,128)(2,1)S(1)}, bf16[128,2048]{1,0:T(8,128)(2,1)}) fusion(f32[1,128,2048]{2,1,0:T(8,128)S(1)} %get-tuple-element.7, f32[2048]{0:T(1024)S(1)} %multiply_multiply_fusion, ...), kind=kLoop, calls=%fused_computation.103 | loop fusion | flops 3145728 | bytes 3678732 | tf_op jit(solution)/shard_map/convert.15
  85.1 0.4 convolution_convert_fusion.2
  85.6 0.2 reshape.136
  85.9 0.2 reshape.137
  86.1 0.4 convolution_convert_fusion.1
  86.7 0.2 reshape.138
  86.9 0.2 reshape.139
  87.2 1.5 %convolution_convert_fusion = bf16[256,2048]{1,0:T(8,128)(2,1)S(1)} fusion(bf16[128,2048]{1,0:T(8,128)(2,1)S(1)} %get-tuple-element.14, bf16[128,2048]{1,0:T(8,128)(2,1)} %get-tuple-element.16, bf16[128,128]{1,0:T(8,128)(2,1)S(1)} %get-tuple-element.36, bf16[128,128]{1,0:T(8,128)(2,1)S(1)} %get-tuple-element.33, bf16[128,128]{1,0:T(8,128)(2,1)S(1)} %get-tuple-element.32), kind=kOutput, calls=%fused_computation.16 | convolution fusion | flops 271581184 | bytes 2195456 | tf_op jit(solution)/shard_map/dot_general | solution.py:67
  88.7 0.9 fusion.85
  89.6 0.2 reshape.140
  89.8 1.3 %reshape.141 = bf16[2048,128]{1,0:T(8,128)(2,1)S(1)} reshape(bf16[128,2048]{1,0:T(8,128)(2,1)} %get-tuple-element.22) | data formatting | bytes 1048576 | tf_op jit(solution)/shard_map/reshape | solution.py:73
  91.1 0.4 fusion.43
  91.5 0.4 fusion.50
  92.0 0.4 fusion.57
  92.4 3.0 %fusion.26 = f32[2048,128]{1,0:T(8,128)S(1)} fusion(f32[2048,256]{1,0:T(8,128)S(1)} %fusion.57, f32[2048,256]{1,0:T(8,128)S(1)} %fusion.50, f32[2048,256]{1,0:T(8,128)S(1)} %fusion.43, f32[]{:T(128)} %reduce_sum.9, f32[]{:T(128)} %bitcast.25, f32[]{:T(128)} %bitcast.23, f32[]{:T(128)} %bitcast), kind=kLoop, calls=%fused_computation.50 | loop fusion | flops 3932160 | bytes 7340048 | tf_op jit(solution)/shard_map/div | solution.py:81
  95.6 0.9 multiply_convert_fusion
  (21 shorter events, 1.1 us)
Async XLA Ops:
  0.0 29.4 %collective-permute-start = (bf16[1,128,2048]{2,1,0:T(8,128)(2,1)}, bf16[1,128,2048]{2,1,0:T(8,128)(2,1)S(1)}, u32[]{:S(2)}, u32[]{:S(2)}) collective-permute-start(bf16[1,128,2048]{2,1,0:T(8,128)(2,1)} %param.7), channel_id=1, source_target_pairs={{0,28},{4,0},{8,4},{12,8},{16,12},{20,16},{24,20},{28,24},{1,29},{... | collective-permute-start | bytes 1572872 | tf_op jit(solution)/shard_map/ppermute | solution.py:20
  6.0 23.5 %collective-permute-start.1 = (bf16[1,128,2048]{2,1,0:T(8,128)(2,1)}, bf16[1,128,2048]{2,1,0:T(8,128)(2,1)S(1)}, u32[]{:S(2)}, u32[]{:S(2)}) collective-permute-start(bf16[1,128,2048]{2,1,0:T(8,128)(2,1)} %param.7), channel_id=1, source_target_pairs={{0,24},{4,28},{8,0},{12,4},{16,8},{20,12},{24,16},{28,20},{1,25},{... | collective-permute-start | bytes 1572872 | tf_op jit(solution)/shard_map/ppermute | solution.py:20
  37.5 3.9 %copy-start = (f32[3]{0:T(128)S(1)}, f32[3]{0:T(128)}, u32[]{:S(2)}) copy-start(f32[3]{0:T(128)} %param.11) | copy-start | bytes 40
  37.5 5.3 %copy-start.1 = (f32[3]{0:T(128)S(1)}, f32[3]{0:T(128)}, u32[]{:S(2)}) copy-start(f32[3]{0:T(128)} %param.10) | copy-start | bytes 40
  37.5 6.0 %copy-start.2 = (s32[1,16]{1,0:T(1,128)S(1)}, s32[1,16]{1,0:T(1,128)}, u32[]{:S(2)}) copy-start(s32[1,16]{1,0:T(1,128)} %param.9) | copy-start | bytes 196
  37.5 29.4 %all-to-all-start = ((bf16[4,128,2048]{2,1,0:T(8,128)(2,1)}), bf16[4,128,2048]{2,1,0:T(8,128)(2,1)S(1)}, u32[]{:S(2)}, u32[]{:S(2)}) async-start(bf16[4,128,2048]{2,1,0:T(8,128)(2,1)} %pad_maximum_fusion), calls=%async_computation | async-start | bytes 4194304 | tf_op jit(solution)/shard_map/all_to_all | solution.py:111
where the time goes:
time: 97.2 us; the launch traced here: 96.5 us
  other arithmetic  31.2 us (32%)
  waiting for transfers between devices  22.8 us (23%)
  between operations  20.7 us (21%)
  starting transfers between devices  10.4 us (11%)
  local copies, waits for them, and re-layouts  7.76 us (8%)
  matrix products  3.67 us (4%)
    all_to_all x1, waiting for transfers between devices, shards(): lax.all_to_all(own_terms, 'dir', split_axis=0, concat_axis=0, tiled=True)  22.8 us
    another operation x3, other arithmetic  18.8 us
    ppermute x2, starting transfers between devices, shifted(): lax.ppermute(value, axis, [(i, (i + by) % count) for i in range(count)])  6.45 us
    add x2, other arithmetic, interpolate(): across = (1.0 - col_frac) * col_first + col_frac * col_second  4.81 us
    all_to_all x1, starting transfers between devices, shards(): lax.all_to_all(own_terms, 'dir', split_axis=0, concat_axis=0, tiled=True)  3.92 us
    div x1, other arithmetic, spots_row(): scaled = spot_sum / jnp.sum(weights)  2.99 us
    another operation x5, other arithmetic, shards(): jnp.stack([shifted_term(extended[0], offset_pairs[target]) for target in...  2.39 us
    dot_general x3, matrix products, spots_row(): jnp.dot(left_table, pupil_field, preferred_element_type=jnp.float32)  2.36 us
  transfers between devices with their start and end apart: 3, of which 1 were waited for; matrix products, arithmetic and copies ran while one was open for 5% of the time, Pallas kernels for 0%

commit v1 on v0

v1 whole, which is shorter than its diff:
```python
import functools
import math

import jax
import jax.numpy as jnp
import numpy as np
from jax import lax
from jax.experimental import pallas as pl
from jax.experimental.pallas import tpu as pltpu
from jax.sharding import PartitionSpec as P

OVER = 2
QUANT = 4
REACH = 2
LANES = 128
CHUNKS = 8
MESH = pl.DeviceIdType.MESH
HALF_PI_HI = 1.5703125
HALF_PI_LO = math.pi / 2 - 1.5703125


def base_tables(n):
    frequency = np.arange(n, dtype=np.float64) - n // 2
    position = np.arange(n, dtype=np.float64) - (n - 1) / 2.0
    angle = -2.0 * math.pi / (OVER * n) * frequency[:, None] * position[None, :]
    factor = 1.0 / math.sqrt(n)
    return (np.cos(angle) * factor).astype(np.float32), (np.sin(angle) * factor).astype(np.float32)


def cos_sin(angle):
    turns = jnp.round(angle * (2.0 / math.pi))
    rest = (angle - turns * HALF_PI_HI) - turns * HALF_PI_LO
    quadrant = turns.astype(jnp.int32)
    square = rest * rest
    sin = rest + rest * square * (-1.0 / 6 + square * (1.0 / 120 - square * (1.0 / 5040)))
    cos = 1.0 + square * (-0.5 + square * (1.0 / 24 - square * (1.0 / 720 - square * (1.0 / 40320))))
    swap = (quadrant & 1) == 1
    cos_value = jnp.where(swap, sin, cos)
    sin_value = jnp.where(swap, cos, sin)
    cos_value = jnp.where(((quadrant + 1) & 2) == 2, -cos_value, cos_value)
    sin_value = jnp.where((quadrant & 2) == 2, -sin_value, sin_value)
    return cos_value, sin_value


def kernel(
    tiles, n, blocks, slices,
    x_ref, off_ref, valid_ref, defocus_ref, weights_ref, fr_ref, fi_ref, right_ref,
    out_ref,
    ext, shifted, mix, slide, send_buf, recv_buf, local, left, col_cos, col_sin,
    z_send, z_recv, s_send, s_recv, o_send, o_recv, p_send, p_recv, y_send, y_recv,
):
    tile = lax.axis_index("tile")
    own = lax.axis_index("dir")
    core = lax.rem(own, 2)
    chip = lax.div(own, 2)
    other_core = chip * 2 + (1 - core)
    other_chip = (1 - chip) * 2 + core
    odd = lax.rem(tile, 2)
    mate = tile + 1 - 2 * odd
    below = lax.rem(tile + tiles - 2, tiles)
    above = lax.rem(tile + 2, tiles)

    barrier = pltpu.get_barrier_semaphore()
    for device in ((tile, other_core), (tile, other_chip), (mate, own), (below, own), (above, own)):
        pl.semaphore_signal(barrier, inc=1, device_id=device, device_id_type=MESH)
    pl.semaphore_wait(barrier, 5)

    rows = n // CHUNKS
    pairs = blocks // 2

    def copy(source, target, send, recv, device):
        return pltpu.make_async_remote_copy(
            src_ref=source, dst_ref=target, send_sem=send, recv_sem=recv,
            device_id=device, device_id_type=MESH,
        )

    def z_copy(k):
        return copy(
            x_ref.at[0, pl.ds(k * rows, rows)], ext.at[core, 2, pl.ds(k * rows, rows)],
            z_send.at[k], z_recv.at[k], (below, own),
        )

    def first_copy(k):
        return copy(
            x_ref.at[0, pl.ds(k * rows, rows)], ext.at[core, 1, pl.ds(k * rows, rows)],
            s_send.at[k], s_recv.at[k], (mate, own),
        )

    def relay_copy(k):
        return copy(
            ext.at[core, 2, pl.ds(k * rows, rows)], ext.at[core, 1, pl.ds(k * rows, rows)],
            s_send.at[k], s_recv.at[k], (mate, own),
        )

    def share_copy(which, k):
        part = ext.at[core, which, pl.ds(k * rows, rows)]
        return copy(part, part, p_send.at[which - 1, k], p_recv.at[which - 1, k], (tile, other_core))

    own_copy = copy(x_ref.at[0], ext.at[core, 0], o_send, o_recv, (tile, other_core))

    for k in range(CHUNKS):
        z_copy(k).start()

        @pl.when(odd == 1)
        def _():
            first_copy(k).start()

    own_copy.start()
    ext[core, 0] = x_ref[0]

    first_row = (tile * n).astype(jnp.float32)
    row_at = lax.broadcasted_iota(jnp.int32, (8, n), 1).astype(jnp.float32)
    p = (first_row + row_at - (tiles * n - 1) / 2.0) / n
    col_at = lax.broadcasted_iota(jnp.int32, (8, blocks * n), 1).astype(jnp.float32)
    q = (col_at - (blocks * n - 1) / 2.0) / n
    for a in range(slices):
        row_cos, row_sin = cos_sin(defocus_ref[a] * (p * p))
        row_cos, row_sin = row_cos[0:1], row_sin[0:1]
        real = fr_ref[...] * row_cos - fi_ref[...] * row_sin
        imag = fr_ref[...] * row_sin + fi_ref[...] * row_cos
        left[2 * a * n : (2 * a + 1) * n, 0:n] = real.astype(jnp.bfloat16)
        left[2 * a * n : (2 * a + 1) * n, n : 2 * n] = (-imag).astype(jnp.bfloat16)
        left[(2 * a + 1) * n : (2 * a + 2) * n, 0:n] = imag.astype(jnp.bfloat16)
        left[(2 * a + 1) * n : (2 * a + 2) * n, n : 2 * n] = real.astype(jnp.bfloat16)
        c, s = cos_sin(defocus_ref[a] * (q * q))
        for j in range(pairs):
            col_cos[j, a] = c[:, j * 2 * n : (j + 1) * 2 * n]
            col_sin[j, a] = s[:, j * 2 * n : (j + 1) * 2 * n]

    def steps_of(direction, slot):
        return off_ref[direction, chip * 2 + slot, 0], off_ref[direction, chip * 2 + slot, 1]

    def taps(shape, shift, fraction, along, across):
        gap = lax.broadcasted_iota(jnp.int32, shape, along) - lax.broadcasted_iota(
            jnp.int32, shape, across
        ) - shift
        return jnp.where(gap == 0, 1.0 - fraction, jnp.where(gap == 1, fraction, 0.0)).astype(
            jnp.bfloat16
        )

    for index, direction in enumerate((other_chip, own)):
        for slot in range(2):
            row_steps, col_steps = steps_of(direction, slot)
            fy = (row_steps & (QUANT - 1)).astype(jnp.float32) * (1.0 / QUANT)
            fx = (col_steps & (QUANT - 1)).astype(jnp.float32) * (1.0 / QUANT)
            down = lax.shift_right_logical(row_steps, 2) & (n - 1)
            over = lax.shift_right_logical(col_steps, 2) & (n - 1)
            mix[index, slot] = taps((n, 2 * n), down, fy, 1, 0)
            tap = taps((3 * n, 2 * n), over, fx, 0, 1)
            for half in range(2):
                first = (slot * 2 + half) * 3 * n
                slide[index, first : first + 3 * n, :] = tap

    for k in range(CHUNKS):
        z_copy(k).wait_recv()
        share_copy(2, k).start()

        @pl.when(odd == 0)
        def _():
            relay_copy(k).start()

        first_copy(k).wait_recv()
        share_copy(1, k).start()
    own_copy.wait_recv()
    for k in range(CHUNKS):
        share_copy(2, k).wait_recv()
        share_copy(1, k).wait_recv()

    def interpolated(index, direction, store, after):
        plans = []
        for slot in range(2):
            row_steps, col_steps = steps_of(direction, slot)
            top = lax.shift_right_logical(row_steps, n.bit_length() + 1)
            plans.append((top, lax.shift_right_logical(col_steps, n.bit_length() + 1)))

        def rows_step(j, carry):
            span = pl.ds(pl.multiple_of(j * 2 * n, 2 * n), 2 * n)
            for slot in range(2):
                top = plans[slot][0]
                window = jnp.concatenate([ext[slot, top, :, span], ext[slot, top + 1, :, span]], 0)
                mixed = jnp.dot(mix[index, slot], window, preferred_element_type=jnp.float32)
                high = mixed.astype(jnp.bfloat16)
                low = (mixed - high.astype(jnp.float32)).astype(jnp.bfloat16)
                for b in range(2):
                    shifted[slot, 0, 2 * j + b] = high[:, b * n : (b + 1) * n]
                    shifted[slot, 1, 2 * j + b] = low[:, b * n : (b + 1) * n]
            return carry

        lax.fori_loop(0, pairs, rows_step, 0)

        def cols_step(j, carry):
            parts = []
            for slot in range(2):
                begin = plans[slot][1] + 2 * j
                for half in range(2):
                    for b in range(3):
                        parts.append(shifted[slot, half, (begin + b) & (blocks - 1)])
            total = jnp.dot(
                jnp.concatenate(parts, 1), slide[index], preferred_element_type=jnp.float32
            )
            store(j, [total[:, :n], total[:, n:]])
            after(j)
            return carry

        lax.fori_loop(0, pairs, cols_step, 0)

    def y_copy(j):
        return copy(send_buf.at[j], recv_buf.at[j], y_send.at[j], y_recv.at[j], (tile, other_chip))

    def store_send(j, total):
        for b in range(2):
            send_buf[j, b] = total[b].astype(jnp.bfloat16)

    def send_previous(j):
        @pl.when(j > 0)
        def _():
            y_copy(j - 1).start()

    def store_local(j, total):
        for b in range(2):
            local[j, b] = total[b]

        @pl.when(j == 0)
        def _():
            y_copy(pairs - 1).start()

    interpolated(0, other_chip, store_send, send_previous)
    interpolated(1, own, store_local, lambda j: None)

    weight_sum = weights_ref[0]
    for a in range(1, slices):
        weight_sum = weight_sum + weights_ref[a]

    def final_step(j, carry):
        y_copy(j).wait_recv()
        fields = []
        for b in range(2):
            c, s = cos_sin(local[j, b] + recv_buf[j, b].astype(jnp.float32))
            fields.append(jnp.concatenate([c, s], 0).astype(jnp.bfloat16))
        field = jnp.concatenate(fields, 1)
        sums = [jnp.zeros((n, n), jnp.float32) for _ in range(2)]
        for a in range(slices):
            focal = jnp.dot(
                left[2 * a * n : (2 * a + 2) * n, :], field, preferred_element_type=jnp.float32
            )
            real, imag = focal[:n], focal[n:]
            c, s = col_cos[j, a][0:1], col_sin[j, a][0:1]
            new_real = (real * c - imag * s).astype(jnp.bfloat16)
            new_imag = (real * s + imag * c).astype(jnp.bfloat16)
            both = jnp.concatenate(
                [
                    jnp.concatenate([new_real[:, b * n : (b + 1) * n], new_imag[:, b * n : (b + 1) * n]], 1)
                    for b in range(2)
                ],
                0,
            )
            spot = jnp.dot(both, right_ref[...], preferred_element_type=jnp.float32)
            power = spot * spot
            for b in range(2):
                piece = power[b * n : (b + 1) * n]
                sums[b] = sums[b] + weights_ref[a] * (piece[:, :n] + piece[:, n:])
        for b in range(2):
            lit = valid_ref[0, 2 * j + b].astype(jnp.float32)
            out_ref[0, 0, :, pl.ds(pl.multiple_of((2 * j + b) * n, n), n)] = (
                sums[b] / weight_sum * lit
            ).astype(jnp.bfloat16)
        return carry

    lax.fori_loop(0, pairs, final_step, 0)

    for k in range(CHUNKS):
        z_copy(k).wait_send()
        first_copy(k).wait_send()
        share_copy(1, k).wait_send()
        share_copy(2, k).wait_send()
    own_copy.wait_send()
    for j in range(pairs):
        y_copy(j).wait_send()


def solution(mesh):
    tiles = mesh.shape["tile"]

    def shards(layers, offsets, subap_valid, defocus, weights):
        n, cols = layers.shape[1], layers.shape[2]
        blocks = cols // n
        slices = defocus.shape[0]
        pairs = blocks // 2
        fr, fi = base_tables(n)
        right = jnp.asarray(np.block([[fr.T, fi.T], [-fi.T, fr.T]])).astype(jnp.bfloat16)
        vmem = pl.BlockSpec(memory_space=pltpu.VMEM)
        smem = pl.BlockSpec(memory_space=pltpu.SMEM)
        dma = pltpu.SemaphoreType.DMA
        return pl.pallas_call(
            functools.partial(kernel, tiles, n, blocks, slices),
            out_shape=jax.ShapeDtypeStruct((1, 1, n, cols), jnp.bfloat16),
            in_specs=[vmem, smem, smem, smem, smem, vmem, vmem, vmem],
            out_specs=vmem,
            scratch_shapes=[
                pltpu.VMEM((2, REACH + 1, n, cols), jnp.bfloat16),
                pltpu.VMEM((2, 2, blocks, n, n), jnp.bfloat16),
                pltpu.VMEM((2, 2, n, 2 * n), jnp.bfloat16),
                pltpu.VMEM((2, 12 * n, 2 * n), jnp.bfloat16),
                pltpu.VMEM((pairs, 2, n, n), jnp.bfloat16),
                pltpu.VMEM((pairs, 2, n, n), jnp.bfloat16),
                pltpu.VMEM((pairs, 2, n, n), jnp.float32),
                pltpu.VMEM((2 * slices * n, 2 * n), jnp.bfloat16),
                pltpu.VMEM((pairs, slices, 8, 2 * n), jnp.float32),
                pltpu.VMEM((pairs, slices, 8, 2 * n), jnp.float32),
                dma((CHUNKS,)), dma((CHUNKS,)),
                dma((CHUNKS,)), dma((CHUNKS,)),
                dma, dma,
                dma((REACH, CHUNKS)), dma((REACH, CHUNKS)),
                dma((pairs,)), dma((pairs,)),
            ],
            compiler_params=pltpu.CompilerParams(collective_id=0, has_side_effects=True),
        )(layers, offsets, subap_valid, defocus, weights, jnp.asarray(fr), jnp.asarray(fi), right)

    placed = (P("dir", "tile", None), P(), P("tile", None), P(), P())
    return jax.shard_map(
        shards, mesh=mesh, in_specs=placed, out_specs=P("dir", "tile", None, None), check_vma=False
    )
```

time: 97.2 us -> 42.3 us (0.44)
  the two profiles are of different devices: /device:TPU:0 before, /device:TPU:3 now
where the time goes in v1:
time: 42.3 us; the launch traced here: 42.1 us
  Pallas kernels  38.8 us (92%)
  local copies, waits for them, and re-layouts  3.26 us (8%)
    pallas_call x1, Pallas kernels, shards(): pl.pallas_call(functools.partial(kernel, tiles, n, blocks, slices), out_s...  38.8 us
    unnamed x2, local copies, waits for them, and re-layouts  3.26 us

profile of v1, /device:TPU:3, one launch (start us, length us, event | category | flops | bytes accessed | tf_op | source)
XLA Modules:
  0.0 42.1 jit_solution(13030016311849492634)
XLA Ops:
  0.0 1.4 %copy.9.off_ref = s32[4,4,2]{2,1,0:T(4,128)} copy(s32[4,4,2]{1,2,0:T(2,128)} %param.9) | data formatting | bytes 256 | tf_op args[1]
  1.4 38.8 %shard_map.82 = bf16[1,1,128,2048]{3,2,1,0:T(8,128)(2,1)} custom-call(bf16[1,128,2048]{2,1,0:T(8,128)(2,1)} %x_ref.1, s32[4,4,2]{2,1,0:T(4,128)} %copy.9.off_ref, s32[1,16]{1,0:T(1,128)} %valid_ref.1, f32[3]{0:T(128)} %defocus_ref.1, f32[3]{0:T(128)} %weights_ref.1, f32[128,128]{1,0:T(8,128)} %constant.7.clone.fr_ref, f32[128,128]{1,0:T(8,128)} %constant.8.clone.fi_ref, ...), custom_call_target="tpu_custom_call" | custom-call | tf_op jit(solution)/shard_map/pallas_call | solution.py:294
  40.2 1.9 %copy.11 = bf16[1,1,128,2048]{3,2,1,0:T(8,128)(2,1)} copy(bf16[1,1,128,2048]{3,2,1,0:T(8,128)(2,1)} %shard_map.82) | data formatting | bytes 1048576

commit v2 on v1

v2 whole, which is shorter than its diff:
```python
import functools
import math

import jax
import jax.numpy as jnp
import numpy as np
from jax import lax
from jax.experimental import pallas as pl
from jax.experimental.pallas import tpu as pltpu
from jax.sharding import PartitionSpec as P

OVER = 2
QUANT = 4
REACH = 2
LANES = 128
CHUNKS = 8
MESH = pl.DeviceIdType.MESH
HALF_PI_HI = 1.5703125
HALF_PI_LO = math.pi / 2 - 1.5703125


def base_tables(n):
    frequency = np.arange(n, dtype=np.float64) - n // 2
    position = np.arange(n, dtype=np.float64) - (n - 1) / 2.0
    angle = -2.0 * math.pi / (OVER * n) * frequency[:, None] * position[None, :]
    factor = 1.0 / math.sqrt(n)
    return (np.cos(angle) * factor).astype(np.float32), (np.sin(angle) * factor).astype(np.float32)


def cos_sin(angle):
    turns = jnp.round(angle * (2.0 / math.pi))
    rest = (angle - turns * HALF_PI_HI) - turns * HALF_PI_LO
    quadrant = turns.astype(jnp.int32)
    square = rest * rest
    sin = rest + rest * square * (-1.0 / 6 + square * (1.0 / 120 - square * (1.0 / 5040)))
    cos = 1.0 + square * (-0.5 + square * (1.0 / 24 - square * (1.0 / 720 - square * (1.0 / 40320))))
    swap = (quadrant & 1) == 1
    cos_value = jnp.where(swap, sin, cos)
    sin_value = jnp.where(swap, cos, sin)
    cos_value = jnp.where(((quadrant + 1) & 2) == 2, -cos_value, cos_value)
    sin_value = jnp.where((quadrant & 2) == 2, -sin_value, sin_value)
    return cos_value, sin_value


def kernel(
    tiles, n, blocks, slices,
    x_ref, off_ref, valid_ref, defocus_ref, weights_ref, fr_ref, fi_ref, right_ref,
    out_ref,
    ext_a, ext_b, ext_far, shifted, mix, slide, send_buf, recv_buf, local, left, col_cos, col_sin,
    z_send, z_recv, s_send, s_recv, o_send, o_recv, r_send, r_recv, p_send, p_recv, y_send, y_recv,
):
    tile = lax.axis_index("tile")
    own = lax.axis_index("dir")
    core = lax.rem(own, 2)
    chip = lax.div(own, 2)
    other_core = chip * 2 + (1 - core)
    other_chip = (1 - chip) * 2 + core
    odd = lax.rem(tile, 2)
    mate = tile + 1 - 2 * odd
    below = lax.rem(tile + tiles - 2, tiles)
    above = lax.rem(tile + 2, tiles)

    barrier = pltpu.get_barrier_semaphore()
    for device in ((tile, other_core), (tile, other_chip), (mate, own), (below, own), (above, own)):
        pl.semaphore_signal(barrier, inc=1, device_id=device, device_id_type=MESH)
    pl.semaphore_wait(barrier, 5)

    ext = (ext_a, ext_b, ext_far)
    rows = n // CHUNKS
    pairs = blocks // 2

    def copy(source, target, send, recv, device):
        return pltpu.make_async_remote_copy(
            src_ref=source, dst_ref=target, send_sem=send, recv_sem=recv,
            device_id=device, device_id_type=MESH,
        )

    def part(slot, which, k):
        return ext[slot].at[which, pl.ds(k * rows, rows)]

    def source(slot, k):
        return part(2, 0, k) if slot == 2 else x_ref.at[0, pl.ds(k * rows, rows)]

    def z_copy(slot, k):
        return copy(
            source(slot, k), part(slot, 2, k), z_send.at[slot, k], z_recv.at[slot, k], (below, own)
        )

    def first_copy(slot, k):
        return copy(
            source(slot, k), part(slot, 1, k), s_send.at[slot, k], s_recv.at[slot, k], (mate, own)
        )

    def relay_copy(slot, k):
        return copy(
            part(slot, 2, k), part(slot, 1, k), s_send.at[slot, k], s_recv.at[slot, k], (mate, own)
        )

    def raw_copy(k):
        return copy(
            x_ref.at[0, pl.ds(k * rows, rows)], part(2, 0, k), r_send.at[k], r_recv.at[k],
            (tile, other_chip),
        )

    def share_copy(slot, which, k):
        return copy(
            part(slot, which, k), part(slot, which, k),
            p_send.at[slot, which, k], p_recv.at[slot, which, k], (tile, other_core),
        )

    def own_copy(slot):
        return copy(x_ref.at[0], ext[slot].at[0], o_send.at[slot], o_recv.at[slot], (tile, other_core))

    def send_halo(slot, k):
        z_copy(slot, k).start()

        @pl.when(odd == 1)
        def _():
            first_copy(slot, k).start()

    def pass_on(slot, k):
        z_copy(slot, k).wait_recv()

        @pl.when(odd == 0)
        def _():
            relay_copy(slot, k).start()

        share_copy(slot, 2, k).start()
        first_copy(slot, k).wait_recv()
        share_copy(slot, 1, k).start()

    def take(slot, k):
        share_copy(slot, 2, k).wait_recv()
        share_copy(slot, 1, k).wait_recv()

    @pl.when(core == 0)
    def _():
        for k in range(CHUNKS):
            send_halo(0, k)
        own_copy(0).start()
        ext_a[0] = x_ref[0]

    @pl.when(core == 1)
    def _():
        for k in range(CHUNKS):
            raw_copy(k).start()
        own_copy(1).start()
        ext_b[0] = x_ref[0]

    first_row = (tile * n).astype(jnp.float32)
    row_at = lax.broadcasted_iota(jnp.int32, (8, n), 1).astype(jnp.float32)
    p = (first_row + row_at - (tiles * n - 1) / 2.0) / n
    col_at = lax.broadcasted_iota(jnp.int32, (8, blocks * n), 1).astype(jnp.float32)
    q = (col_at - (blocks * n - 1) / 2.0) / n
    for a in range(slices):
        row_cos, row_sin = cos_sin(defocus_ref[a] * (p * p))
        row_cos, row_sin = row_cos[0:1], row_sin[0:1]
        real = fr_ref[...] * row_cos - fi_ref[...] * row_sin
        imag = fr_ref[...] * row_sin + fi_ref[...] * row_cos
        left[2 * a * n : (2 * a + 1) * n, 0:n] = real.astype(jnp.bfloat16)
        left[2 * a * n : (2 * a + 1) * n, n : 2 * n] = (-imag).astype(jnp.bfloat16)
        left[(2 * a + 1) * n : (2 * a + 2) * n, 0:n] = imag.astype(jnp.bfloat16)
        left[(2 * a + 1) * n : (2 * a + 2) * n, n : 2 * n] = real.astype(jnp.bfloat16)
        c, s = cos_sin(defocus_ref[a] * (q * q))
        for j in range(pairs):
            col_cos[j, a] = c[:, j * 2 * n : (j + 1) * 2 * n]
            col_sin[j, a] = s[:, j * 2 * n : (j + 1) * 2 * n]

    def taps(shape, shift, fraction, along, across):
        gap = lax.broadcasted_iota(jnp.int32, shape, along) - lax.broadcasted_iota(
            jnp.int32, shape, across
        ) - shift
        return jnp.where(gap == 0, 1.0 - fraction, jnp.where(gap == 1, fraction, 0.0)).astype(
            jnp.bfloat16
        )

    layer_a, layer_b, layer_far = chip * 2, chip * 2 + 1, (1 - chip) * 2 + 1
    terms = ((other_chip, layer_a), (own, layer_a), (own, layer_b), (own, layer_far))
    slots = (0, 0, 1, 2)
    tops, begins = [], []
    for term, (direction, layer) in enumerate(terms):
        row_steps, col_steps = off_ref[direction, 0, layer], off_ref[direction, 1, layer]
        tops.append(lax.shift_right_logical(row_steps, n.bit_length() + 1))
        begins.append(lax.shift_right_logical(col_steps, n.bit_length() + 1))
        fy = (row_steps & (QUANT - 1)).astype(jnp.float32) * (1.0 / QUANT)
        fx = (col_steps & (QUANT - 1)).astype(jnp.float32) * (1.0 / QUANT)
        down = lax.shift_right_logical(row_steps, 2) & (n - 1)
        over = lax.shift_right_logical(col_steps, 2) & (n - 1)
        mix[term] = taps((n, 2 * n), down, fy, 1, 0)
        tap = taps((3 * n, 2 * n), over, fx, 0, 1)
        slide[6 * term * n : (6 * term + 3) * n, :] = tap
        slide[(6 * term + 3) * n : (6 * term + 6) * n, :] = tap

    def rows_step(term, j):
        span = pl.ds(pl.multiple_of(j * 2 * n, 2 * n), 2 * n)
        slot, top = slots[term], tops[term]
        window = jnp.concatenate([ext[slot][top, :, span], ext[slot][top + 1, :, span]], 0)
        mixed = jnp.dot(mix[term], window, preferred_element_type=jnp.float32)
        high = mixed.astype(jnp.bfloat16)
        low = (mixed - high.astype(jnp.float32)).astype(jnp.bfloat16)
        for b in range(2):
            shifted[term, 0, 2 * j + b] = high[:, b * n : (b + 1) * n]
            shifted[term, 1, 2 * j + b] = low[:, b * n : (b + 1) * n]

    def cols_step(first, last, j):
        parts = []
        for term in range(first, last):
            begin = begins[term] + 2 * j
            for half in range(2):
                for b in range(3):
                    parts.append(shifted[term, half, (begin + b) & (blocks - 1)])
        return jnp.dot(
            jnp.concatenate(parts, 1), slide[6 * first * n : 6 * last * n, :],
            preferred_element_type=jnp.float32,
        )

    def y_copy(j):
        return copy(send_buf.at[j], recv_buf.at[j], y_send.at[j], y_recv.at[j], (tile, other_chip))

    def loop(body):
        def step(j, carry):
            body(j)
            return carry

        lax.fori_loop(0, pairs, step, 0)

    @pl.when(core == 0)
    def _():
        loop(lambda k: pass_on(0, k))

    @pl.when(core == 1)
    def _():
        own_copy(0).wait_recv()
        for k in range(CHUNKS // 2):
            take(0, k)
        for k in range(CHUNKS):
            send_halo(1, k)
        for k in range(CHUNKS):
            raw_copy(k).wait_recv()
            share_copy(2, 0, k).start()
            send_halo(2, k)
        for k in range(CHUNKS // 2, CHUNKS):
            take(0, k)

    loop(lambda j: rows_step(0, j))

    def send_step(j):
        send_buf[j] = cols_step(0, 1, j).astype(jnp.bfloat16)

        @pl.when(j > 0)
        def _():
            y_copy(j - 1).start()

    loop(send_step)

    def near_step(j):
        rows_step(1, j)

        @pl.when(j == 0)
        def _():
            y_copy(pairs - 1).start()

        @pl.when(core == 0)
        def _():
            take(1, j)

        @pl.when(core == 1)
        def _():
            pass_on(1, j)

    loop(near_step)

    @pl.when(core == 0)
    def _():
        own_copy(1).wait_recv()

    def far_step(j):
        rows_step(2, j)
        local[j] = cols_step(1, 2, j)

        @pl.when(core == 0)
        def _():
            share_copy(2, 0, j).wait_recv()
            take(2, j)

        @pl.when(core == 1)
        def _():
            pass_on(2, j)

    loop(far_step)
    loop(lambda j: rows_step(3, j))

    weight_sum = weights_ref[0]
    for a in range(1, slices):
        weight_sum = weight_sum + weights_ref[a]

    def final_step(j, carry):
        y_copy(j).wait_recv()
        phase = local[j] + cols_step(2, 4, j) + recv_buf[j].astype(jnp.float32)
        field = jnp.concatenate(cos_sin(phase), 0).astype(jnp.bfloat16)
        sums = [jnp.zeros((n, n), jnp.float32) for _ in range(2)]
        for a in range(slices):
            focal = jnp.dot(
                left[2 * a * n : (2 * a + 2) * n, :], field, preferred_element_type=jnp.float32
            )
            real, imag = focal[:n], focal[n:]
            c, s = col_cos[j, a][0:1], col_sin[j, a][0:1]
            new_real = (real * c - imag * s).astype(jnp.bfloat16)
            new_imag = (real * s + imag * c).astype(jnp.bfloat16)
            both = jnp.concatenate(
                [
                    jnp.concatenate([new_real[:, b * n : (b + 1) * n], new_imag[:, b * n : (b + 1) * n]], 1)
                    for b in range(2)
                ],
                0,
            )
            spot = jnp.dot(both, right_ref[...], preferred_element_type=jnp.float32)
            power = spot * spot
            for b in range(2):
                piece = power[b * n : (b + 1) * n]
                sums[b] = sums[b] + weights_ref[a] * (piece[:, :n] + piece[:, n:])
        for b in range(2):
            lit = valid_ref[0, 2 * j + b].astype(jnp.float32)
            out_ref[0, 0, :, pl.ds(pl.multiple_of((2 * j + b) * n, n), n)] = (
                sums[b] / weight_sum * lit
            ).astype(jnp.bfloat16)
        return carry

    lax.fori_loop(0, pairs, final_step, 0)

    def finish(slot):
        own_copy(slot).wait_send() if slot < 2 else None
        for k in range(CHUNKS):
            z_copy(slot, k).wait_send()
            first_copy(slot, k).wait_send()
            share_copy(slot, 1, k).wait_send()
            share_copy(slot, 2, k).wait_send()
            if slot == 2:
                share_copy(slot, 0, k).wait_send()
                raw_copy(k).wait_send()

    @pl.when(core == 0)
    def _():
        finish(0)

    @pl.when(core == 1)
    def _():
        finish(1)
        finish(2)

    for j in range(pairs):
        y_copy(j).wait_send()


def solution(mesh):
    tiles = mesh.shape["tile"]

    def shards(layers, offsets, subap_valid, defocus, weights):
        n, cols = layers.shape[1], layers.shape[2]
        blocks = cols // n
        slices = defocus.shape[0]
        pairs = blocks // 2
        fr, fi = base_tables(n)
        right = jnp.asarray(np.block([[fr.T, fi.T], [-fi.T, fr.T]])).astype(jnp.bfloat16)
        vmem = pl.BlockSpec(memory_space=pltpu.VMEM)
        smem = pl.BlockSpec(memory_space=pltpu.SMEM)
        dma = pltpu.SemaphoreType.DMA
        return pl.pallas_call(
            functools.partial(kernel, tiles, n, blocks, slices),
            out_shape=jax.ShapeDtypeStruct((1, 1, n, cols), jnp.bfloat16),
            in_specs=[vmem, smem, smem, smem, smem, vmem, vmem, vmem],
            out_specs=vmem,
            scratch_shapes=[
                pltpu.VMEM((REACH + 1, n, cols), jnp.bfloat16),
                pltpu.VMEM((REACH + 1, n, cols), jnp.bfloat16),
                pltpu.VMEM((REACH + 1, n, cols), jnp.bfloat16),
                pltpu.VMEM((4, 2, blocks, n, n), jnp.bfloat16),
                pltpu.VMEM((4, n, 2 * n), jnp.bfloat16),
                pltpu.VMEM((24 * n, 2 * n), jnp.bfloat16),
                pltpu.VMEM((pairs, n, 2 * n), jnp.bfloat16),
                pltpu.VMEM((pairs, n, 2 * n), jnp.bfloat16),
                pltpu.VMEM((pairs, n, 2 * n), jnp.float32),
                pltpu.VMEM((2 * slices * n, 2 * n), jnp.bfloat16),
                pltpu.VMEM((pairs, slices, 8, 2 * n), jnp.float32),
                pltpu.VMEM((pairs, slices, 8, 2 * n), jnp.float32),
                dma((3, CHUNKS)), dma((3, CHUNKS)),
                dma((3, CHUNKS)), dma((3, CHUNKS)),
                dma((2,)), dma((2,)),
                dma((CHUNKS,)), dma((CHUNKS,)),
                dma((3, REACH + 1, CHUNKS)), dma((3, REACH + 1, CHUNKS)),
                dma((pairs,)), dma((pairs,)),
            ],
            compiler_params=pltpu.CompilerParams(collective_id=0, has_side_effects=True),
        )(layers, jnp.transpose(offsets, (0, 2, 1)), subap_valid, defocus, weights, jnp.asarray(fr), jnp.asarray(fi), right)

    placed = (P("dir", "tile", None), P(), P("tile", None), P(), P())
    return jax.shard_map(
        shards, mesh=mesh, in_specs=placed, out_specs=P("dir", "tile", None, None), check_vma=False
    )
```

time: 42.3 us -> 47.3 us (1.12); the launches traced: 42.1 us -> 46.6 us
  Pallas kernels: 38.8 us -> 44.7 us
  local copies, waits for them, and re-layouts: 3.26 us -> 1.88 us
    pallas_call x1, Pallas kernels: 38.8 us -> 44.7 us  [shards(): pl.pallas_call(functools.partial(kernel, tiles, n, blocks, slices), out_s...]
    unnamed x2 -> x1, local copies, waits for them, and re-layouts: 3.26 us -> 1.88 us
where the time goes in v2:
time: 47.3 us; the launch traced here: 46.6 us
  Pallas kernels  44.7 us (95%)
  local copies, waits for them, and re-layouts  1.88 us (4%)
    pallas_call x1, Pallas kernels, shards(): pl.pallas_call(functools.partial(kernel, tiles, n, blocks, slices), out_s...  44.7 us
    unnamed x1, local copies, waits for them, and re-layouts  1.88 us

profile of v2, /device:TPU:3, one launch (start us, length us, event | category | flops | bytes accessed | tf_op | source)
XLA Modules:
  0.0 46.6 jit_solution(13471184883873550297)
XLA Ops:
  0.0 44.7 %shard_map.82 = bf16[1,1,128,2048]{3,2,1,0:T(8,128)(2,1)} custom-call(bf16[1,128,2048]{2,1,0:T(8,128)(2,1)} %x_ref.1, s32[4,2,4]{2,1,0:T(2,128)} %bitcast.1, s32[1,16]{1,0:T(1,128)} %valid_ref.1, f32[3]{0:T(128)} %defocus_ref.1, f32[3]{0:T(128)} %weights_ref.1, f32[128,128]{1,0:T(8,128)} %constant.7.clone.fr_ref, f32[128,128]{1,0:T(8,128)} %constant.8.clone.fi_ref, ...), custom_call_target="tpu_custom_call" | custom-call | tf_op jit(solution)/shard_map/pallas_call | solution.py:368
  44.7 1.9 %copy.10 = bf16[1,1,128,2048]{3,2,1,0:T(8,128)(2,1)} copy(bf16[1,1,128,2048]{3,2,1,0:T(8,128)(2,1)} %shard_map.82) | data formatting | bytes 1048576

commit v3 on v1

--- a/solution.py
+++ b/solution.py
@@ -128,7 +128,7 @@
             col_sin[j, a] = s[:, j * 2 * n : (j + 1) * 2 * n]
 
     def steps_of(direction, slot):
-        return off_ref[direction, chip * 2 + slot, 0], off_ref[direction, chip * 2 + slot, 1]
+        return off_ref[direction, 0, chip * 2 + slot], off_ref[direction, 1, chip * 2 + slot]
 
     def taps(shape, shift, fraction, along, across):
         gap = lax.broadcasted_iota(jnp.int32, shape, along) - lax.broadcasted_iota(
@@ -186,7 +186,7 @@
                     shifted[slot, 1, 2 * j + b] = low[:, b * n : (b + 1) * n]
             return carry
 
-        lax.fori_loop(0, pairs, rows_step, 0)
+        lax.fori_loop(0, pairs, rows_step, 0, unroll=4)
 
         def cols_step(j, carry):
             parts = []
@@ -202,7 +202,7 @@
             after(j)
             return carry
 
-        lax.fori_loop(0, pairs, cols_step, 0)
+        lax.fori_loop(0, pairs, cols_step, 0, unroll=2)
 
     def y_copy(j):
         return copy(send_buf.at[j], recv_buf.at[j], y_send.at[j], y_recv.at[j], (tile, other_chip))
@@ -266,7 +266,7 @@
             ).astype(jnp.bfloat16)
         return carry
 
-    lax.fori_loop(0, pairs, final_step, 0)
+    lax.fori_loop(0, pairs, final_step, 0, unroll=2)
 
     for k in range(CHUNKS):
         z_copy(k).wait_send()
@@ -314,7 +314,7 @@
                 dma((pairs,)), dma((pairs,)),
             ],
             compiler_params=pltpu.CompilerParams(collective_id=0, has_side_effects=True),
-        )(layers, offsets, subap_valid, defocus, weights, jnp.asarray(fr), jnp.asarray(fi), right)
+        )(layers, jnp.transpose(offsets, (0, 2, 1)), subap_valid, defocus, weights, jnp.asarray(fr), jnp.asarray(fi), right)
 
     placed = (P("dir", "tile", None), P(), P("tile", None), P(), P())
     return jax.shard_map(

time: 42.3 us -> 40.1 us (0.948)
  local copies, waits for them, and re-layouts: 3.26 us -> 1.88 us
  Pallas kernels: 38.8 us -> 38 us
    unnamed x2 -> x1, local copies, waits for them, and re-layouts: 3.26 us -> 1.88 us
    pallas_call x1, Pallas kernels: 38.8 us -> 38 us  [shards(): pl.pallas_call(functools.partial(kernel, tiles, n, blocks, slices), out_s...]
where the time goes in v3:
time: 40.1 us; the launch traced here: 39.9 us
  Pallas kernels  38 us (95%)
  local copies, waits for them, and re-layouts  1.88 us (5%)
    pallas_call x1, Pallas kernels, shards(): pl.pallas_call(functools.partial(kernel, tiles, n, blocks, slices), out_s...  38 us
    unnamed x1, local copies, waits for them, and re-layouts  1.88 us

profile of v3, /device:TPU:3, one launch (start us, length us, event | category | flops | bytes accessed | tf_op | source)
XLA Modules:
  0.0 39.9 jit_solution(17651969129899497013)
XLA Ops:
  0.0 38.0 %shard_map.82 = bf16[1,1,128,2048]{3,2,1,0:T(8,128)(2,1)} custom-call(bf16[1,128,2048]{2,1,0:T(8,128)(2,1)} %x_ref.1, s32[4,2,4]{2,1,0:T(2,128)} %bitcast.1, s32[1,16]{1,0:T(1,128)} %valid_ref.1, f32[3]{0:T(128)} %defocus_ref.1, f32[3]{0:T(128)} %weights_ref.1, f32[128,128]{1,0:T(8,128)} %constant.7.clone.fr_ref, f32[128,128]{1,0:T(8,128)} %constant.8.clone.fi_ref, ...), custom_call_target="tpu_custom_call" | custom-call | tf_op jit(solution)/shard_map/pallas_call | solution.py:294
  38.0 1.9 %copy.10 = bf16[1,1,128,2048]{3,2,1,0:T(8,128)(2,1)} copy(bf16[1,1,128,2048]{3,2,1,0:T(8,128)(2,1)} %shard_map.82) | data formatting | bytes 1048576
